TPU v7x, 32 devices: a whole 2x2x4 slice. The times are simulated.
32 devices in a mesh: row: 16 (over z, y, core), col: 2 (over x).
Axes of the slice: x: 2, y: 2, z: 4, core: 2. Of those that a mesh axis runs over, the one named last changes fastest.
Arguments:
- images: bfloat16 [2048, 1024], P(('row', 'col')), as said below
- texts: bfloat16 [2048, 1024], P(('row', 'col')), as said below
- matches: int32 [2048], P('row'), may hold values from 0 to 2047, each once
- logit_scale: float32 [], replicated, may hold values from 20 to 400
Outputs:
- loss: float32 [], replicated
- image_grad: float32 [2048, 1024], P(('row', 'col'))
- text_grad: float32 [2048, 1024], P(('row', 'col'))
Inputs may be any that keep to these rules, and one draw needn't show every extreme that they name: `images`: each row is a float embedding whose entries are not all zero. `texts`: each row is a float embedding of order one. `matches`: a permutation of the 2048 text indices.
All inputs are finite; a program needn't handle non-finite values.
Results may differ from a plain program's by a relative error of at most 0.0015.
The roundings to bfloat16 on the way count: a program that leaves them out, or rounds other values in their place, can miss the bound.
Values may be sent and summed in bfloat16 or wider, within the bound.
A program may use at most 128 MiB of HBM per device.

v0:
```python
import jax
import jax.numpy as jnp
from jax import lax
from jax.sharding import PartitionSpec as P

EPSILON = 1e-06


def merged(value, axis, join):
    pieces = jax.tree.map(lambda part: lax.all_gather(part, axis), value)
    head = jax.tree.map(lambda part: part[0], pieces)
    tail = jax.tree.map(lambda part: part[1:], pieces)
    running, _ = lax.scan(lambda running, piece: (join(running, piece), None), head, tail)
    return running


def unit_rows(values):
    wide = values.astype(jnp.float32)
    norms = jnp.sqrt(jnp.sum(wide * wide, axis=1, keepdims=True) + EPSILON)
    return (wide / norms, norms)


def back_unit(unit, norms, grad):
    inner = jnp.sum(unit * grad, axis=1, keepdims=True)
    return (grad - unit * inner) / norms


def combine_stats(first, second):
    top = jnp.maximum(first[0], second[0])
    return (top, first[1] * jnp.exp(first[0] - top) + second[1] * jnp.exp(second[0] - top))


def on_device(images, texts, matches, logit_scale):
    per_dev = images.shape[0]
    n_row = lax.axis_size("row")
    n_col = lax.axis_size("col")
    total = per_dev * n_row * n_col
    col_pos = lax.axis_index("col")
    row_pos = lax.axis_index("row")
    image_unit, image_norm = unit_rows(images)
    text_unit, text_norm = unit_rows(texts)
    image_low = image_unit.astype(jnp.bfloat16)
    text_low = text_unit.astype(jnp.bfloat16)
    image_rows = lax.all_gather(image_low, "col", axis=0, tiled=True)
    half = 0
    stride = 1
    n_img = image_rows.shape[0]

    def scores_of(piece):
        return logit_scale * lax.dot_general(
            piece, image_rows, (((1,), (1,)), ((), ())), preferred_element_type=jnp.float32
        )

    def match_mask(count):
        place = jnp.arange(count, dtype=jnp.int32)
        owner = place // per_dev * stride + half
        text_ids = owner * (n_col * per_dev) + col_pos * per_dev + place % per_dev
        return text_ids[:, None] == matches[None, :]

    piece = lax.all_gather(text_low, "row", axis=0, tiled=True)
    row_max = jnp.full((n_img,), -jnp.inf, jnp.float32)
    row_sum = jnp.zeros((n_img,), jnp.float32)
    scores = scores_of(piece)
    top = jnp.max(scores, axis=0)
    row_sum = row_sum * jnp.exp(row_max - top) + jnp.sum(jnp.exp(scores - top[None, :]), axis=0)
    piece_max = jnp.max(scores, axis=1)
    piece_sum = jnp.sum(jnp.exp(scores - piece_max[:, None]), axis=1)
    col_max = piece_max
    col_sum = piece_sum
    mask = match_mask(piece.shape[0])
    matched = jnp.sum(jnp.where(mask, scores, jnp.float32(0.0)))
    stats = (top, row_sum, col_max, col_sum, matched)
    row_max, row_sum, col_max, col_sum, matched = stats
    row_max, row_sum = merged((row_max, row_sum), "col", combine_stats)
    slot_max = col_max
    slot_sum = col_sum
    slot_max, slot_sum = merged((slot_max, slot_sum), "row", combine_stats)
    col_max = slot_max
    col_sum = slot_sum
    row_lse = row_max + jnp.log(row_sum)
    col_lse = col_max + jnp.log(col_sum)
    own_rows = jnp.sum(
        lax.dynamic_slice_in_dim(row_lse, (half * n_col + col_pos) * per_dev, per_dev, 0)
    )
    own_cols = jnp.sum(lax.dynamic_slice_in_dim(col_lse, row_pos // stride * per_dev, per_dev, 0))
    share = (own_rows + own_cols) / (2.0 * total) - matched / total
    loss = lax.psum(share, ("row", "col"))
    piece = lax.all_gather(text_low, "row", axis=0, tiled=True)
    count = piece.shape[0]
    scores = scores_of(piece)
    mask = match_mask(count).astype(jnp.float32)
    weights = (
        0.5 * jnp.exp(scores - row_lse[None, :]) + 0.5 * jnp.exp(scores - col_lse[:, None]) - mask
    )
    weights = (logit_scale * weights).astype(jnp.bfloat16)
    image_acc = lax.dot_general(
        weights, piece, (((0,), (0,)), ((), ())), preferred_element_type=jnp.float32
    )
    text_piece = jnp.dot(weights, image_rows, preferred_element_type=jnp.float32)
    text_acc = text_piece
    image_acc, text_acc = (image_acc, text_acc)
    image_unit_grad = lax.psum_scatter(image_acc, "col", scatter_dimension=0, tiled=True)
    text_unit_grad = lax.psum_scatter(text_acc, "row", scatter_dimension=0, tiled=True)
    image_grad = back_unit(image_unit, image_norm, image_unit_grad)
    text_grad = back_unit(text_unit, text_norm, text_unit_grad)
    return (loss, image_grad, text_grad)


def solution(mesh):
    placed = (P(("row", "col"), None), P(("row", "col"), None), P("row"), P())
    return jax.shard_map(
        on_device,
        mesh=mesh,
        in_specs=placed,
        out_specs=(P(), P(("row", "col"), None), P(("row", "col"), None)),
        check_vma=False,
    )
```

profile of v0, /device:TPU:0, one launch (start us, length us, event | category | flops | bytes accessed | tf_op | source)
XLA Modules:
  0.0 206.4 jit_solution(2421729306633929638)
XLA Ops:
  7.2 0.0 copy-start.3
  7.2 0.0 all-gather.7.cloned.1.call-start
  7.2 1.0 fusion.4
  8.3 1.7 fusion.29
  9.9 0.0 all-gather.7.cloned.1.call-update
  10.0 0.0 reduce-scatter.3.cloned.1.call-start
  10.7 1.0 fusion.5
  11.7 1.0 fusion.30
  12.7 7.1 %all_gather.30 = bf16[128,1024]{1,0:T(8,128)(2,1)S(1)} all-gather(bf16[64,1024]{1,0:T(8,128)(2,1)S(1)} %fusion.30), channel_id=1, replica_groups=mesh['row'=16,'col'=2] {'col'}, dimensions={0}, use_global_device_ids=true | all-gather | bytes 393216 | tf_op jit(solution)/shard_map/all_gather | solution.py:44
  19.8 35.1 %all-gather.7.cloned.1.call-done = bf16[1024,1024]{1,0:T(8,128)(2,1)} async-done(((bf16[64,1024]{1,0:T(8,128)(2,1)}), bf16[1024,1024]{1,0:T(8,128)(2,1)}) %all-gather.7.cloned.1.call-update) | async-done | bytes 2097168 | tf_op jit(solution)/shard_map/all_gather | solution.py:60
  54.9 0.0 copy-start
  54.9 2.5 %fusion.35 = (f32[1024]{0:T(1024)S(1)}, f32[128]{0:T(128)S(1)}, f32[1024,128]{1,0:T(8,128)S(1)}) fusion(bf16[1024,1024]{1,0:T(8,128)(2,1)} %all-gather.7.cloned.1.call-done, bf16[128,1024]{1,0:T(8,128)(2,1)S(1)} %all_gather.30, f32[]{:T(128)S(6)} %copy.16), kind=kOutput, calls=%fused_computation.67 | convolution fusion | flops 268827520 | bytes 2888196 | tf_op jit(solution)/shard_map/dot_general | solution.py:50
  57.5 0.0 copy-done.3
  57.5 1.0 fusion
  58.5 19.3 %all-gather.2 = f32[16384]{0:T(1024)S(1)} all-gather(f32[1024]{0:T(1024)S(1)} %get-tuple-element.49), channel_id=4, replica_groups=mesh['row'=16,'col'=2] {'row'}, dimensions={0}, use_global_device_ids=true | all-gather | bytes 69632 | tf_op jit(solution)/shard_map/all_gather | solution.py:10
  77.8 17.6 %all-gather.1 = f32[16384]{0:T(1024)S(1)} all-gather(f32[1024]{0:T(1024)S(1)} %get-tuple-element.51), channel_id=3, replica_groups=mesh['row'=16,'col'=2] {'row'}, dimensions={0}, use_global_device_ids=true | all-gather | bytes 69632 | tf_op jit(solution)/shard_map/all_gather | solution.py:10
  95.4 4.2 %all-gather.3 = f32[2,1,128]{2,1,0:T(1,128)S(1)} all-gather(f32[1,1,128]{2,1,0:T(1,128)S(1)} %bitcast.83), channel_id=2, replica_groups=mesh['row'=16,'col'=2] {'col'}, dimensions={0}, use_global_device_ids=true | all-gather | bytes 1536 | tf_op jit(solution)/shard_map/all_gather | solution.py:10
  99.6 4.2 %all-gather.4 = f32[2,1,128]{2,1,0:T(1,128)S(1)} all-gather(f32[1,1,128]{2,1,0:T(1,128)S(1)} %add_bitcast_fusion), channel_id=1, replica_groups=mesh['row'=16,'col'=2] {'col'}, dimensions={0}, use_global_device_ids=true | all-gather | bytes 1536 | tf_op jit(solution)/shard_map/all_gather | solution.py:10
  103.9 0.8 while.2
  104.7 0.0 copy-done
  104.7 1.8 fusion.33
  106.6 0.0 reduce-scatter.3.cloned.1.call-update
  106.6 0.0 reduce-scatter.5.cloned.1.call-start
  106.6 2.7 %fusion.31 = f32[1024,1024]{1,0:T(8,128)} fusion(bf16[128,1024]{1,0:T(8,128)(2,1)S(1)} %all_gather.30, f32[1024,128]{1,0:T(8,128)S(1)} %get-tuple-element.67, f32[1024]{0:T(1024)S(1)} %log_add_fusion, f32[128]{0:T(128)S(1)} %fusion.28, s32[128]{0:T(128)S(1)} %copy-done.3, f32[]{:T(128)S(6)} %copy.16, s32[1024]{0:T(1024)S(1)} %fusion.14), kind=kOutput, calls=%fused_computation.65 | convolution fusion | flops 269615104 | bytes 4989956 | tf_op jit(solution)/shard_map/dot_general | solution.py:99
  109.3 0.0 copy-start.1
  109.3 0.0 copy-start.2
  109.3 0.0 reduce-scatter.5.cloned.1.call-update
  109.4 0.7 dynamic-slice_reduce_fusion
  110.7 0.7 dynamic-slice_reduce_fusion.1
  112.7 38.0 %psum.7 = f32[]{:T(128)} all-reduce(f32[]{:T(128)S(6)} %sub.94), channel_id=1, replica_groups=mesh['row'=16,'col'=2] {'row','col'}, use_global_device_ids=true, to_apply=%region_11.12 | all-reduce | flops 1 | bytes 8 | tf_op jit(solution)/shard_map/psum | solution.py:87
  150.7 0.0 reduce-scatter.3.cloned.1.call-done
  150.7 0.0 copy-done.1
  150.7 1.2 multiply_reduce_fusion.1
  151.9 1.8 subtract_divide_fusion.1
  153.7 43.2 %reduce-scatter.5.cloned.1.call-done = f32[64,1024]{1,0:T(8,128)} async-done(((f32[1024,1024]{1,0:T(8,128)}), f32[64,1024]{1,0:T(8,128)}) %reduce-scatter.5.cloned.1.call-update) | async-done | bytes 262160 | tf_op jit(solution)/shard_map/reduce_scatter | solution.py:103
  196.9 0.0 copy-done.2
  196.9 1.2 multiply_reduce_fusion
  198.1 1.8 subtract_divide_fusion
  (43 shorter events, 0.5 us)
Async XLA Ops:
  7.2 50.3 %copy-start.3 = (s32[128]{0:T(128)S(1)}, s32[128]{0:T(128)}, u32[]{:S(2)}) copy-start(s32[128]{0:T(128)} %param.8) | copy-start | bytes 1540
  7.2 47.8 %all-gather.7.cloned.1.call-start = ((), (), s32[]{:S(2)}) async-start(), calls=%async_computation.2 | async-start | bytes 2228224 | tf_op jit(solution)/shard_map/all_gather | solution.py:60
  10.0 140.8 %reduce-scatter.3.cloned.1.call-start = ((), (), s32[]{:S(2)}) async-start(), calls=%async_computation.3 | async-start | bytes 786432 | tf_op jit(solution)/shard_map/reduce_scatter | solution.py:102
  54.9 49.8 %copy-start = (bf16[1024,1024]{1,0:T(8,128)(2,1)S(1)}, bf16[1024,1024]{1,0:T(8,128)(2,1)}, u32[]{:S(2)}) copy-start(bf16[1024,1024]{1,0:T(8,128)(2,1)} %all-gather.7.cloned.1.call-done) | copy-start | bytes 6291460
  106.6 90.3 %reduce-scatter.5.cloned.1.call-start = ((), (), s32[]{:S(2)}) async-start(), calls=%async_computation.4 | async-start | bytes 4456448 | tf_op jit(solution)/shard_map/reduce_scatter | solution.py:103
  109.3 41.4 %copy-start.1 = (bf16[64,1024]{1,0:T(8,128)(2,1)S(1)}, bf16[64,1024]{1,0:T(8,128)(2,1)}, u32[]{:S(2)}) copy-start(bf16[64,1024]{1,0:T(8,128)(2,1)} %param.6) | copy-start | bytes 393220
  109.3 87.6 %copy-start.2 = (bf16[64,1024]{1,0:T(8,128)(2,1)S(1)}, bf16[64,1024]{1,0:T(8,128)(2,1)}, u32[]{:S(2)}) copy-start(bf16[64,1024]{1,0:T(8,128)(2,1)} %param.7) | copy-start | bytes 393220
Sparse Core Ops, SparseCore 0:
  10.7 44.1 all-gather.6
  106.7 13.2 reduce-scatter.2
  123.9 72.9 reduce-scatter.4
where the time goes:
time: 207 us; the launch traced here: 206 us
  blocking collectives  90.5 us (44%)
  waiting for transfers between devices  78.4 us (38%)
  between operations  16.5 us (8%)
  other arithmetic  13.2 us (6%)
  matrix products  7.05 us (3%)
    all_gather x4, blocking collectives, merged(): pieces = jax.tree.map(lambda part: lax.all_gather(part, axis), value)  45.3 us
    reduce_scatter x1, waiting for transfers between devices, on_device(): lax.psum_scatter(text_acc, 'row', scatter_dimension=0, tiled=True)  43.2 us
    psum x1, blocking collectives, on_device(): loss = lax.psum(share, ('row', 'col'))  38 us
    all_gather x1, waiting for transfers between devices, on_device(): piece = lax.all_gather(text_low, 'row', axis=0, tiled=True)  35.1 us
    all_gather x1, blocking collectives, on_device(): image_rows = lax.all_gather(image_low, 'col', axis=0, tiled=True)  7.12 us
  transfers between devices with their start and end apart: 3, of which 2 were waited for; matrix products, arithmetic and copies ran while one was open for 4% of the time, Pallas kernels for 0%

commit v1 on v0

--- a/solution.py
+++ b/solution.py
@@ -1,9 +1,14 @@
+import functools
+
 import jax
 import jax.numpy as jnp
 from jax import lax
+from jax.experimental import pallas as pl
+from jax.experimental.pallas import tpu as pltpu
 from jax.sharding import PartitionSpec as P
 
 EPSILON = 1e-06
+MESH = pl.DeviceIdType.MESH
 
 
 def merged(value, axis, join):
@@ -106,10 +111,272 @@
     return (loss, image_grad, text_grad)
 
 
+def fused_kernel(
+    n_row, n_col, img_ref, txt_ref, match_ref, scale_ref, loss_ref, gimg_ref, gtxt_ref,
+    raw, low, own, sc, ex, wbuf, stat, tile, lsem, ssem, rsem,
+):
+    per = img_ref.shape[0]
+    n_dev = n_row * n_col
+    total = per * n_dev
+    units = raw.shape[1]
+    width = 4 * per
+    pair = 2 * per
+    row = lax.axis_index("row")
+    x = lax.axis_index("col")
+    z, y, c = row // 4, (row // 2) % 2, row % 2
+    me = row * n_col + x
+    scale = scale_ref[0, 0]
+
+    def place(zz, yy, cc, xx):
+        return ((zz * 4 + yy * 2 + cc), xx)
+
+    barrier = pltpu.get_barrier_semaphore()
+    peers = [(me + k) % n_dev for k in range(1, n_dev)]
+    peers = [(p // n_col, p % n_col) for p in peers]
+    for peer in peers:
+        pl.semaphore_signal(barrier, inc=1, device_id=peer, device_id_type=MESH)
+
+    inputs = (img_ref, txt_ref)
+    kept = [
+        pltpu.make_async_copy(inputs[a], raw.at[a, z * 2 + y, c * 2 + x], lsem.at[a])
+        for a in range(2)
+    ]
+    for copy in kept:
+        copy.start()
+    for a in range(2):
+        wide = inputs[a][...].astype(jnp.float32)
+        norm = jnp.sqrt(jnp.sum(wide * wide, axis=1, keepdims=True) + EPSILON)
+        own[a] = (wide * (1.0 / norm)).astype(jnp.bfloat16)
+    for copy in kept:
+        copy.wait()
+    pl.semaphore_wait(barrier, n_dev - 1)
+
+    copies = []
+
+    def send(src, dst, target):
+        k = len(copies)
+        copy = pltpu.make_async_remote_copy(
+            src_ref=src, dst_ref=dst, send_sem=ssem.at[k], recv_sem=rsem.at[k],
+            device_id=target, device_id_type=MESH,
+        )
+        copy.start()
+        copies.append(copy)
+        return copy
+
+    def move(a, zz, yy, xx, target):
+        ref = raw.at[a, zz * 2 + yy, c * 2 + xx]
+        return send(ref, ref, target)
+
+    to_x, to_y = place(z, y, c, 1 - x), place(z, 1 - y, c, x)
+    sibling = place(z, y, 1 - c, x)
+
+    def share(zz, yy, xx):
+        ref = raw.at[:, zz * 2 + yy, c * 2 + xx]
+        return send(ref, ref, sibling)
+
+    def zmate(k):
+        low_bit, high_bit = z % 2, z // 2
+        if k & 1:
+            low_bit = 1 - low_bit
+        if k & 2:
+            high_bit = 1 - high_bit
+        return high_bit * 2 + low_bit
+
+    zs = [zmate(k) for k in range(4)]
+
+    def process(zz, yy):
+        unit = zz * 2 + yy
+        for a in range(2):
+            @pl.loop(0, 4)
+            def _(b):
+                wide = raw[a, unit, b].astype(jnp.float32)
+                norm = jnp.sqrt(jnp.sum(wide * wide, axis=1, keepdims=True) + EPSILON)
+                rows = pl.ds(pl.multiple_of(unit * width + b * per, per), per)
+                low[a, rows, :] = (wide * (1.0 / norm)).astype(jnp.bfloat16)
+
+            rows = pl.ds(pl.multiple_of(unit * width, width), width)
+            sc[a, unit] = scale * lax.dot_general(
+                own[1 - a], low[a, rows, :], (((1,), (1,)), ((), ())),
+                preferred_element_type=jnp.float32,
+            )
+
+    lines = [None]
+    first, second, third, shares = {}, {}, {}, {}
+
+    def stage1(k):
+        if k:
+            for copy in lines[k]:
+                copy.wait_recv()
+        ax = move(0, zs[k], y, x, to_x)
+        by = move(1, zs[k], y, x, to_y)
+        bx = move(1, zs[k], y, x, to_x)
+        ay = move(0, zs[k], y, x, to_y)
+        first[k] = (ax, by)
+        second[k] = (bx, ay)
+        shares[k] = [share(zs[k], y, x)]
+
+    def stage2(k):
+        ax, by = first[k]
+        ax.wait_recv()
+        ady = move(0, zs[k], y, 1 - x, to_y)
+        by.wait_recv()
+        bdx = move(1, zs[k], 1 - y, x, to_x)
+        third[k] = (ady, bdx)
+
+    def stage3(k):
+        bx, ay = second[k]
+        bx.wait_recv()
+        shares[k].append(share(zs[k], y, 1 - x))
+        ay.wait_recv()
+        shares[k].append(share(zs[k], 1 - y, x))
+
+    def stage4(k):
+        for copy in third[k]:
+            copy.wait_recv()
+        shares[k].append(share(zs[k], 1 - y, 1 - x))
+
+    stage1(0)
+    for k in range(1, 4):
+        lines.append([move(a, z, y, x, place(zs[k], y, c, x)) for a in range(2)])
+    stage2(0)
+    for k in range(4):
+        if k + 1 < 4:
+            stage1(k + 1)
+        stage3(k)
+        shares[k][0].wait_recv()
+        shares[k][1].wait_recv()
+        process(zs[k], y)
+        stage4(k)
+        if k + 1 < 4:
+            stage2(k + 1)
+        shares[k][2].wait_recv()
+        shares[k][3].wait_recv()
+        process(zs[k], 1 - y)
+
+    lane = lax.broadcasted_iota(jnp.int32, (per, pair), 1)
+    sub = lax.broadcasted_iota(jnp.int32, (per, pair), 0)
+    eye = lane == sub + x * per
+    match_row = match_ref[...].astype(jnp.float32)
+    match_own = jnp.sum(jnp.where(eye, match_row, 0.0), axis=1, keepdims=True)
+    lses, sums = [None, None], [None, None]
+    for a in range(2):
+        top = jnp.max(sc[a, 0], axis=1, keepdims=True)
+        for u in range(1, units):
+            top = jnp.maximum(top, jnp.max(sc[a, u], axis=1, keepdims=True))
+        acc = jnp.zeros((per, width), jnp.float32)
+        for u in range(units):
+            e = jnp.exp(sc[a, u] - top)
+            ex[a, u] = e
+            acc = acc + e
+        sums[a] = jnp.sum(acc, axis=1, keepdims=True)
+        lses[a] = top + jnp.log(sums[a])
+    unit_lane = lax.broadcasted_iota(jnp.int32, (per, width), 1).astype(jnp.float32)
+    hit = jnp.zeros((per, width), jnp.float32)
+    for u in range(units):
+        hit = hit + jnp.where(unit_lane + float(u * width) == match_own, sc[1, u], 0.0)
+    matched = jnp.sum(jnp.sum(hit, axis=1, keepdims=True), axis=0, keepdims=True)
+
+    def as_lanes(column):
+        return jnp.sum(jnp.where(eye, column, 0.0), axis=0, keepdims=True)
+
+    here = lax.broadcasted_iota(jnp.int32, (1, pair), 1)
+    inside = (here >= x * per) & (here < (x + 1) * per)
+    tile[0:1, :] = as_lanes(lses[1])
+    tile[1:2, :] = as_lanes(lses[0])
+    tile[2:3, :] = jnp.where(inside, match_row, 0.0)
+    tile[3:4, :] = jnp.where(here == 0, matched, 0.0)
+    tile[4:8, :] = jnp.zeros((4, pair), jnp.float32)
+    stat[me] = tile[...]
+    news = [send(tile, stat.at[me], peer) for peer in peers]
+
+    for a in range(2):
+        half = 0.5 / sums[a]
+        for u in range(units):
+            part = ex[a, u] * half
+            if a == 1:
+                part = part - jnp.where(unit_lane + float(u * width) == match_own, 1.0, 0.0)
+            ex[a, u] = part
+
+    for copy in news:
+        copy.wait_recv()
+    blocks = [stat[2 * k] + stat[2 * k + 1] for k in range(n_dev // 2)]
+    everyone = blocks[0]
+    for block in blocks[1:]:
+        everyone = everyone + block
+    rows8 = lax.broadcasted_iota(jnp.int32, everyone.shape, 0)
+    factor = jnp.where(rows8 < 2, 0.5 / total, jnp.where(rows8 == 3, -1.0 / total, 0.0))
+    loss_ref[...] = jnp.sum(
+        jnp.sum(everyone * factor, axis=1, keepdims=True), axis=0, keepdims=True
+    )
+    text_id = (
+        lax.broadcasted_iota(jnp.int32, (per, 1), 0) + me * per
+    ).astype(jnp.float32)
+    for a in (1, 0):
+        for u in range(units):
+            wide = jnp.concatenate([blocks[2 * u], blocks[2 * u + 1]], axis=1)
+            other = wide[1:2, :] if a == 1 else wide[0:1, :]
+            value = ex[a, u] + 0.5 * jnp.exp(sc[a, u] - other)
+            if a == 0:
+                value = value - jnp.where(wide[2:3, :] == text_id, 1.0, 0.0)
+            wbuf[a, :, u * width : (u + 1) * width] = (scale * value).astype(jnp.bfloat16)
+        grad = jnp.dot(wbuf[a], low[a], preferred_element_type=jnp.float32)
+        source, out = (img_ref, gimg_ref) if a == 1 else (txt_ref, gtxt_ref)
+        wide = source[...].astype(jnp.float32)
+        norm = jnp.sqrt(jnp.sum(wide * wide, axis=1, keepdims=True) + EPSILON)
+        inv = 1.0 / norm
+        unit = wide * inv
+        inner = jnp.sum(unit * grad, axis=1, keepdims=True)
+        out[...] = (grad - unit * inner) * inv
+    for copy in copies:
+        copy.wait_send()
+
+
+def fused(n_row, n_col, images, texts, matches, logit_scale):
+    per, d = images.shape
+    n_dev = n_row * n_col
+    units = n_dev // 4
+    n_sem = 6 + 10 * 4 + n_dev - 1
+    vmem = pl.BlockSpec(memory_space=pltpu.VMEM)
+    loss, image_grad, text_grad = pl.pallas_call(
+        functools.partial(fused_kernel, n_row, n_col),
+        out_shape=(
+            jax.ShapeDtypeStruct((1, 1), jnp.float32),
+            jax.ShapeDtypeStruct((per, d), jnp.float32),
+            jax.ShapeDtypeStruct((per, d), jnp.float32),
+        ),
+        in_specs=[vmem, vmem, vmem, pl.BlockSpec(memory_space=pltpu.SMEM)],
+        out_specs=(vmem, vmem, vmem),
+        scratch_shapes=[
+            pltpu.VMEM((2, units, 4, per, d), jnp.bfloat16),
+            pltpu.VMEM((2, units * 4 * per, d), jnp.bfloat16),
+            pltpu.VMEM((2, per, d), jnp.bfloat16),
+            pltpu.VMEM((2, units, per, 4 * per), jnp.float32),
+            pltpu.VMEM((2, units, per, 4 * per), jnp.float32),
+            pltpu.VMEM((2, per, units * 4 * per), jnp.bfloat16),
+            pltpu.VMEM((n_dev, 8, 2 * per), jnp.float32),
+            pltpu.VMEM((8, 2 * per), jnp.float32),
+            pltpu.SemaphoreType.DMA((2,)),
+            pltpu.SemaphoreType.DMA((n_sem,)),
+            pltpu.SemaphoreType.DMA((n_sem,)),
+        ],
+        compiler_params=pltpu.CompilerParams(
+            collective_id=0, has_side_effects=True, vmem_limit_bytes=56 * 1024 * 1024
+        ),
+    )(images, texts, matches.reshape(1, -1), logit_scale.reshape(1, 1))
+    return loss.reshape(()), image_grad, text_grad
+
+
 def solution(mesh):
     placed = (P(("row", "col"), None), P(("row", "col"), None), P("row"), P())
+    n_row, n_col = mesh.shape["row"], mesh.shape["col"]
+
+    def body(images, texts, matches, logit_scale):
+        if n_col == 2 and n_row == 16 and matches.shape[0] == 128:
+            return fused(n_row, n_col, images, texts, matches, logit_scale)
+        return on_device(images, texts, matches, logit_scale)
+
     return jax.shard_map(
-        on_device,
+        body,
         mesh=mesh,
         in_specs=placed,
         out_specs=(P(), P(("row", "col"), None), P(("row", "col"), None)),

time: 207 us -> 65.9 us (0.32)
  blocking collectives: 90.5 us -> 0 us
  waiting for transfers between devices: 78.4 us -> 0 us
  Pallas kernels: 0 us -> 60.2 us
  between operations: 16.5 us -> 3.06 us
  other arithmetic: 13.2 us -> 0 us
  matrix products: 7.05 us -> 0 us
  local copies, waits for them, and re-layouts: 0.27 us -> 2.42 us
    pallas_call x0 -> x1, Pallas kernels: none -> 60.2 us  [fused(): pl.pallas_call(functools.partial(fused_kernel, n_row, n_col), out_shape=(...]
    all_gather x5 -> x0, blocking collectives: 52.5 us -> none  [the longest x4 45.3 us: merged(): pieces = jax.tree.map(lambda part: lax.all_gather(part, axis), value)]
    reduce_scatter x2 -> x0, waiting for transfers between devices: 43.2 us -> none  [the longest x1 43.2 us: on_device(): lax.psum_scatter(text_acc, 'row', scatter_dimension=0, tiled=True)]
    psum x1 -> x0, blocking collectives: 38 us -> none  [on_device(): loss = lax.psum(share, ('row', 'col'))]
    all_gather x1 -> x0, waiting for transfers between devices: 35.1 us -> none  [on_device(): piece = lax.all_gather(text_low, 'row', axis=0, tiled=True)]
    dot_general x3 -> x0, matrix products: 7.05 us -> none  [the longest x1 2.7 us: on_device(): jnp.dot(weights, image_rows, preferred_element_type=jnp.float32)]
    reduce_sum x7 -> x0, other arithmetic: 6.72 us -> none  [the longest x2 2.31 us: back_unit(): inner = jnp.sum(unit * grad, axis=1, keepdims=True)]
    div x2 -> x0, other arithmetic: 3.55 us -> none  [back_unit(): return (grad - unit * inner) / norms]
  transfers between devices with their start and end apart: 3 -> 0, of which waited for: 2 -> 0; matrix products, arithmetic and copies ran while one was open for 4% -> 0% of each run, Pallas kernels for 0% -> 0%
where the time goes in v1:
time: 65.9 us; the launch traced here: 65.7 us
  Pallas kernels  60.2 us (91%)
  between operations  3.06 us (5%)
  local copies, waits for them, and re-layouts  2.42 us (4%)
    pallas_call x1, Pallas kernels, fused(): pl.pallas_call(functools.partial(fused_kernel, n_row, n_col), out_shape=(...  60.2 us
    unnamed x4, local copies, waits for them, and re-layouts  2.42 us

profile of v1, /device:TPU:0, one launch (start us, length us, event | category | flops | bytes accessed | tf_op | source)
XLA Modules:
  0.0 65.7 jit_solution(3203823159749355498)
XLA Ops:
  1.3 60.2 %shard_map.67 = (f32[1,1]{1,0:T(1,128)}, f32[64,1024]{1,0:T(8,128)}, f32[64,1024]{1,0:T(8,128)}) custom-call(bf16[64,1024]{1,0:T(8,128)(2,1)} %img_ref.1, bf16[64,1024]{1,0:T(8,128)(2,1)} %txt_ref.1, s32[1,128]{1,0:T(1,128)} %bitcast.4, f32[1,1]{1,0:T(1,128)} %bitcast.3.scale_ref), custom_call_target="tpu_custom_call" | custom-call | tf_op jit(solution)/shard_map/pallas_call | solution.py:340
  62.1 0.0 copy-start
  62.2 1.7 %copy.12 = f32[64,1024]{1,0:T(8,128)} copy(f32[64,1024]{1,0:T(8,128)} %get-tuple-element.13) | data formatting | bytes 524288
  63.9 0.0 copy-done
  63.9 0.7 %copy.13 = f32[64,1024]{1,0:T(8,128)} copy(f32[64,1024]{1,0:T(8,128)S(1)} %copy-done) | data formatting | bytes 524288
Async XLA Ops:
  62.1 1.7 %copy-start = (f32[64,1024]{1,0:T(8,128)S(1)}, f32[64,1024]{1,0:T(8,128)}, u32[]{:S(2)}) copy-start(f32[64,1024]{1,0:T(8,128)} %get-tuple-element.14) | copy-start | bytes 786436

commit v2 on v1

--- a/solution.py
+++ b/solution.py
@@ -133,7 +133,8 @@
     barrier = pltpu.get_barrier_semaphore()
     peers = [(me + k) % n_dev for k in range(1, n_dev)]
     peers = [(p // n_col, p % n_col) for p in peers]
-    for peer in peers:
+    greet = [(row,1-x),(z*4+(1-y)*2+c,x),(z*4+y*2+1-c,x)]+[(((z+k)%4)*4+y*2+c,x) for k in (1,2,3)]
+    for peer in greet:
         pl.semaphore_signal(barrier, inc=1, device_id=peer, device_id_type=MESH)
 
     inputs = (img_ref, txt_ref)
@@ -149,7 +150,7 @@
         own[a] = (wide * (1.0 / norm)).astype(jnp.bfloat16)
     for copy in kept:
         copy.wait()
-    pl.semaphore_wait(barrier, n_dev - 1)
+    pl.semaphore_wait(barrier, len(greet))
 
     copies = []
 

time: 65.9 us -> 63.8 us (0.968)
  Pallas kernels: 60.2 us -> 58.2 us
    pallas_call x1, Pallas kernels: 60.2 us -> 58.2 us  [fused(): pl.pallas_call(functools.partial(fused_kernel, n_row, n_col), out_shape=(...]
where the time goes in v2:
time: 63.8 us; the launch traced here: 63.7 us
  Pallas kernels  58.2 us (91%)
  between operations  3.06 us (5%)
  local copies, waits for them, and re-layouts  2.42 us (4%)
    pallas_call x1, Pallas kernels, fused(): pl.pallas_call(functools.partial(fused_kernel, n_row, n_col), out_shape=(...  58.2 us
    unnamed x4, local copies, waits for them, and re-layouts  2.42 us

profile of v2, /device:TPU:0, one launch (start us, length us, event | category | flops | bytes accessed | tf_op | source)
XLA Modules:
  0.0 63.7 jit_solution(9605995667808825273)
XLA Ops:
  1.3 58.2 %shard_map.67 = (f32[1,1]{1,0:T(1,128)}, f32[64,1024]{1,0:T(8,128)}, f32[64,1024]{1,0:T(8,128)}) custom-call(bf16[64,1024]{1,0:T(8,128)(2,1)} %img_ref.1, bf16[64,1024]{1,0:T(8,128)(2,1)} %txt_ref.1, s32[1,128]{1,0:T(1,128)} %bitcast.4, f32[1,1]{1,0:T(1,128)} %bitcast.3.scale_ref), custom_call_target="tpu_custom_call" | custom-call | tf_op jit(solution)/shard_map/pallas_call | solution.py:341
  60.1 0.0 copy-start
  60.1 1.7 %copy.12 = f32[64,1024]{1,0:T(8,128)} copy(f32[64,1024]{1,0:T(8,128)} %get-tuple-element.13) | data formatting | bytes 524288
  61.8 0.0 copy-done
  61.8 0.7 %copy.13 = f32[64,1024]{1,0:T(8,128)} copy(f32[64,1024]{1,0:T(8,128)S(1)} %copy-done) | data formatting | bytes 524288
Async XLA Ops:
  60.1 1.7 %copy-start = (f32[64,1024]{1,0:T(8,128)S(1)}, f32[64,1024]{1,0:T(8,128)}, u32[]{:S(2)}) copy-start(f32[64,1024]{1,0:T(8,128)} %get-tuple-element.14) | copy-start | bytes 786436

commit v3 on v2

--- a/solution.py
+++ b/solution.py
@@ -187,15 +187,16 @@
 
     def process(zz, yy):
         unit = zz * 2 + yy
-        for a in range(2):
-            @pl.loop(0, 4)
-            def _(b):
+        @pl.loop(0, 4)
+        def _(b):
+            for a in range(2):
                 wide = raw[a, unit, b].astype(jnp.float32)
                 norm = jnp.sqrt(jnp.sum(wide * wide, axis=1, keepdims=True) + EPSILON)
                 rows = pl.ds(pl.multiple_of(unit * width + b * per, per), per)
                 low[a, rows, :] = (wide * (1.0 / norm)).astype(jnp.bfloat16)
 
-            rows = pl.ds(pl.multiple_of(unit * width, width), width)
+        rows = pl.ds(pl.multiple_of(unit * width, width), width)
+        for a in range(2):
             sc[a, unit] = scale * lax.dot_general(
                 own[1 - a], low[a, rows, :], (((1,), (1,)), ((), ())),
                 preferred_element_type=jnp.float32,
@@ -217,6 +218,8 @@
         shares[k] = [share(zs[k], y, x)]
 
     def stage2(k):
+        if k == 1:
+            return
         ax, by = first[k]
         ax.wait_recv()
         ady = move(0, zs[k], y, 1 - x, to_y)
@@ -225,6 +228,9 @@
         third[k] = (ady, bdx)
 
     def stage3(k):
+        if k == 1:
+            for copy in first[k]:
+                copy.wait_recv()
         bx, ay = second[k]
         bx.wait_recv()
         shares[k].append(share(zs[k], y, 1 - x))
@@ -234,6 +240,9 @@
     def stage4(k):
         for copy in third[k]:
             copy.wait_recv()
+        if k == 0:
+            corner = raw.at[:, z * 2 + 1 - y, c * 2 + 1 - x]
+            third[1] = (send(corner, corner, place(zs[1], y, c, x)),)
         shares[k].append(share(zs[k], 1 - y, 1 - x))
 
     stage1(0)

time: 63.8 us -> 60.2 us (0.944)
  Pallas kernels: 58.2 us -> 54.5 us
    pallas_call x1, Pallas kernels: 58.2 us -> 54.5 us  [fused(): pl.pallas_call(functools.partial(fused_kernel, n_row, n_col), out_shape=(...]
where the time goes in v3:
time: 60.2 us; the launch traced here: 60 us
  Pallas kernels  54.5 us (91%)
  between operations  3.06 us (5%)
  local copies, waits for them, and re-layouts  2.42 us (4%)
    pallas_call x1, Pallas kernels, fused(): pl.pallas_call(functools.partial(fused_kernel, n_row, n_col), out_shape=(...  54.5 us
    unnamed x4, local copies, waits for them, and re-layouts  2.42 us

profile of v3, /device:TPU:0, one launch (start us, length us, event | category | flops | bytes accessed | tf_op | source)
XLA Modules:
  0.0 60.0 jit_solution(12416117119019945446)
XLA Ops:
  1.3 54.5 %shard_map.67 = (f32[1,1]{1,0:T(1,128)}, f32[64,1024]{1,0:T(8,128)}, f32[64,1024]{1,0:T(8,128)}) custom-call(bf16[64,1024]{1,0:T(8,128)(2,1)} %img_ref.1, bf16[64,1024]{1,0:T(8,128)(2,1)} %txt_ref.1, s32[1,128]{1,0:T(1,128)} %bitcast.4, f32[1,1]{1,0:T(1,128)} %bitcast.3.scale_ref), custom_call_target="tpu_custom_call" | custom-call | tf_op jit(solution)/shard_map/pallas_call | solution.py:350
  56.4 0.0 copy-start
  56.4 1.7 %copy.12 = f32[64,1024]{1,0:T(8,128)} copy(f32[64,1024]{1,0:T(8,128)} %get-tuple-element.13) | data formatting | bytes 524288
  58.2 0.0 copy-done
  58.2 0.7 %copy.13 = f32[64,1024]{1,0:T(8,128)} copy(f32[64,1024]{1,0:T(8,128)S(1)} %copy-done) | data formatting | bytes 524288
Async XLA Ops:
  56.4 1.7 %copy-start = (f32[64,1024]{1,0:T(8,128)S(1)}, f32[64,1024]{1,0:T(8,128)}, u32[]{:S(2)}) copy-start(f32[64,1024]{1,0:T(8,128)} %get-tuple-element.14) | copy-start | bytes 786436

commit v4 on v3

--- a/solution.py
+++ b/solution.py
@@ -183,7 +183,7 @@
             high_bit = 1 - high_bit
         return high_bit * 2 + low_bit
 
-    zs = [zmate(k) for k in range(4)]
+    zs = [zmate(k) for k in (0, 1, 3, 2)]
 
     def process(zz, yy):
         unit = zz * 2 + yy

time: 60.2 us -> 59.3 us (0.985)
  Pallas kernels: 54.5 us -> 53.6 us
    pallas_call x1, Pallas kernels: 54.5 us -> 53.6 us  [fused(): pl.pallas_call(functools.partial(fused_kernel, n_row, n_col), out_shape=(...]
where the time goes in v4:
time: 59.3 us; the launch traced here: 59.1 us
  Pallas kernels  53.6 us (90%)
  between operations  3.06 us (5%)
  local copies, waits for them, and re-layouts  2.42 us (4%)
    pallas_call x1, Pallas kernels, fused(): pl.pallas_call(functools.partial(fused_kernel, n_row, n_col), out_shape=(...  53.6 us
    unnamed x4, local copies, waits for them, and re-layouts  2.42 us

profile of v4, /device:TPU:0, one launch (start us, length us, event | category | flops | bytes accessed | tf_op | source)
XLA Modules:
  0.0 59.1 jit_solution(10487801191524532009)
XLA Ops:
  1.3 53.6 %shard_map.67 = (f32[1,1]{1,0:T(1,128)}, f32[64,1024]{1,0:T(8,128)}, f32[64,1024]{1,0:T(8,128)}) custom-call(bf16[64,1024]{1,0:T(8,128)(2,1)} %img_ref.1, bf16[64,1024]{1,0:T(8,128)(2,1)} %txt_ref.1, s32[1,128]{1,0:T(1,128)} %bitcast.4, f32[1,1]{1,0:T(1,128)} %bitcast.3.scale_ref), custom_call_target="tpu_custom_call" | custom-call | tf_op jit(solution)/shard_map/pallas_call | solution.py:350
  55.5 0.0 copy-start
  55.6 1.7 %copy.12 = f32[64,1024]{1,0:T(8,128)} copy(f32[64,1024]{1,0:T(8,128)} %get-tuple-element.13) | data formatting | bytes 524288
  57.3 0.0 copy-done
  57.3 0.7 %copy.13 = f32[64,1024]{1,0:T(8,128)} copy(f32[64,1024]{1,0:T(8,128)S(1)} %copy-done) | data formatting | bytes 524288
Async XLA Ops:
  55.5 1.7 %copy-start = (f32[64,1024]{1,0:T(8,128)S(1)}, f32[64,1024]{1,0:T(8,128)}, u32[]{:S(2)}) copy-start(f32[64,1024]{1,0:T(8,128)} %get-tuple-element.14) | copy-start | bytes 786436
